TPU v7x, 256 devices: a whole 4x4x8 slice. The times are simulated.
256 devices in a mesh: leaf: 8 (over y, core), wide: 32 (over x, z).
Axes of the slice: x: 4, y: 4, z: 8, core: 2. Of those that a mesh axis runs over, the one named last changes fastest.
Arguments:
- rhs: float32 [262144, 256], P(('leaf', 'wide')), may hold values from -6 to 6
- points: float32 [262144, 128], P(('leaf', 'wide')), may hold values from -6 to 6
- order: int32 [262144], P(('leaf', 'wide')), may hold values from 0 to 1023, as said below
- basis: float32 [262144, 256], P(('leaf', 'wide')), may hold values from -0.1875 to 0.1875
- transfer: float32 [256, 256, 256], P(('leaf', 'wide')), may hold values from -0.125 to 0.125
- skeleton: float32 [32, 256, 128], P('wide', 'leaf'), may hold values from -6 to 6
- far_ids: int32 [32, 6], replicated, may hold values from 0 to 31, as said below
- far_count: int32 [32], replicated, may hold values from 1 to 6
- near_ids: int32 [256, 2], P(('leaf', 'wide')), may hold values from 0 to 255, as said below
- near_count: int32 [256], P(('leaf', 'wide')), may hold values from 0 to 2
Outputs:
- product: float32 [262144, 256], P(('leaf', 'wide'))
Inputs may be any that keep to these rules, and one draw needn't show every extreme that they name: `order`: within each leaf, the 1024 values are a permutation of 0 to 1023. `far_ids`: the first far_count[p] entries of row p are distinct parents other than p; later entries equal p. `near_ids`: the first near_count[g] entries of row g are distinct and each is g - 1 or g + 1 with the same leaf position, that is, a leaf of the parent beside g's parent; g - 1 comes first; later entries equal g.
All inputs are finite; a program needn't handle non-finite values.
Results may differ from a plain program's by a relative error of at most 0.0003.
Values sent between devices are 32-bit elements; how exact they have to be, the bound alone decides.
A program may use at most 64 MiB of HBM per device.

v0:
```python
import jax
import jax.numpy as jnp
from jax import lax
from jax.sharding import PartitionSpec as P

HIGH = lax.Precision.HIGHEST


def split_up(x, dim, size):
    before, after = (x.shape[:dim], x.shape[dim + 1 :])
    return jnp.moveaxis(x.reshape(*before, size, -1, *after), dim, 0)


def sent_and_summed(x, axis, dim):
    size = lax.axis_size(axis)
    blocks = lax.all_to_all(split_up(x, dim, size), axis, 0, 0, tiled=True)
    return jnp.sum(blocks, axis=0)


def side_by_side(arrays, axis, dim, along):
    both = jnp.concatenate(arrays, axis=along)
    out, at, gathered = (lax.all_gather(both, axis, axis=dim, tiled=True), 0, [])
    for a in arrays:
        gathered.append(lax.slice_in_dim(out, at, at + a.shape[along], axis=along))
        at += a.shape[along]
    return tuple(gathered)


def total_of_pieces(x, axis):
    blocks = lax.all_gather(x, axis)
    return blocks.sum(axis=0)


def passed_along(block, axis, distance):
    devices = range(lax.axis_size(axis))
    route = [(i - distance, i) for i in devices if i - distance in devices]
    return lax.ppermute(block, axis, route)


def multiply(left, right):
    return lax.dot_general(
        left, right, (((1,), (0,)), ((), ())), precision=HIGH, preferred_element_type=jnp.float32
    )


def multiply_first(left, right):
    return lax.dot_general(
        left, right, (((0,), (0,)), ((), ())), precision=HIGH, preferred_element_type=jnp.float32
    )


def kernel_tile(left, right):
    cross = lax.dot_general(
        left, right, (((1,), (1,)), ((), ())), precision=HIGH, preferred_element_type=jnp.float32
    )
    sq_left = jnp.sum(left * left, axis=1)
    sq_right = jnp.sum(right * right, axis=1)
    return jnp.exp(-2.0 / left.shape[1] * (sq_left[:, None] + sq_right[None, :] - 2.0 * cross))


def far_terms(targets, sources, coefs, far_row, far_used):
    total = jnp.zeros((targets.shape[0], coefs.shape[2]), jnp.float32)
    for slot in range(far_row.shape[0]):
        other = far_row[slot]
        term = multiply(kernel_tile(targets, sources[other]), coefs[other])
        total = total + jnp.where(slot < far_used, term, jnp.float32(0.0))
    return total


def shards(rhs, points, order, basis, transfer, skeleton, far_ids, far_count, near_ids, near_count):
    wide_count = lax.axis_size("wide")
    parent = lax.axis_index("wide")
    leaf_number = lax.axis_index("leaf") * wide_count + parent
    tree_rhs = rhs[order]
    own_transfer = transfer[0]
    leaf_coef = multiply_first(basis, tree_rhs)
    far_row = far_ids[parent]
    far_used = far_count[parent]
    coef_rows = sent_and_summed(multiply_first(own_transfer, leaf_coef), "leaf", 0)
    skel_full = lax.all_gather(skeleton[0], "leaf", axis=0, tiled=True)
    all_coef, all_skel = side_by_side((coef_rows[None], skeleton), "wide", 0, 2)
    partial_field = far_terms(skel_full, all_skel, all_coef, far_row, far_used)
    field = total_of_pieces(partial_field, "leaf")
    far_out = multiply(basis, multiply(own_transfer, field))
    near_row = near_ids[0]
    used = jnp.arange(near_row.shape[0], dtype=jnp.int32) < near_count[0]
    has_left = jnp.any(used & (near_row == leaf_number - 1))
    has_right = jnp.any(used & (near_row == leaf_number + 1))
    total = multiply(kernel_tile(points, points), tree_rhs)
    right_points, right_rhs = passed_along((points, tree_rhs), "wide", -1)
    pair_tile = kernel_tile(points, right_points)
    total = total + jnp.where(has_right, multiply(pair_tile, right_rhs), jnp.float32(0.0))
    returned = multiply_first(pair_tile, tree_rhs)
    left_share = passed_along(returned, "wide", 1)
    total = total + jnp.where(has_left, left_share, jnp.float32(0.0))
    tree_out = total + far_out
    return jnp.zeros_like(rhs).at[order].set(tree_out)


def solution(mesh):
    placed = (
        P(("leaf", "wide"), None),
        P(("leaf", "wide"), None),
        P(("leaf", "wide")),
        P(("leaf", "wide"), None),
        P(("leaf", "wide"), None, None),
        P("wide", "leaf", None),
        P(),
        P(),
        P(("leaf", "wide"), None),
        P(("leaf", "wide")),
    )
    return jax.shard_map(
        shards, mesh=mesh, in_specs=placed, out_specs=P(("leaf", "wide"), None), check_vma=False
    )
```

profile of v0, /device:TPU:2, one launch (start us, length us, event | category | flops | bytes accessed | tf_op | source)
XLA Modules:
  0.0 183.0 jit_solution(380767807477499763)
XLA Ops:
  6.5 0.8 broadcast_clamp_fusion
  7.3 4.7 %gather_fusion = f32[1024,256]{1,0:T(8,128)S(1)} fusion(f32[1024,256]{1,0:T(8,128)} %param.10, s32[1024]{0:T(1024)S(1)} %get-tuple-element.19), kind=kCustom, calls=%fused_computation | custom fusion | bytes 2101248 | tf_op jit(solution)/shard_map/gather | solution.py:74
  12.1 1.8 fusion.119
  13.9 0.6 fusion.57
  14.5 11.8 %all_to_all.5 = f32[8,32,256]{2,1,0:T(8,128)S(1)} all-to-all(f32[8,32,256]{2,1,0:T(8,128)S(1)} %bitcast.172), channel_id=1, replica_groups=mesh['leaf'=8,'wide'=32] {'leaf'}, dimensions={0} | all-to-all | bytes 524288 | tf_op jit(solution)/shard_map/all_to_all | solution.py:16
  26.3 0.6 pad_maximum_fusion
  27.0 0.0 all-gather.5.cloned.1.call-update
  27.0 0.0 all-gather.7.cloned.1.call-start
  27.1 0.1 constant_dynamic-slice_fusion
  27.1 0.6 fusion.116
  35.3 0.6 dynamic_slice.42
  43.5 12.8 %all-gather = f32[1,256,128]{2,1,0:T(8,128)S(1)} all-gather(f32[1,32,128]{2,1,0:T(8,128)S(1)} %copy-done.4), channel_id=2, replica_groups=mesh['leaf'=8,'wide'=32] {'leaf'}, dimensions={1}, use_global_device_ids=true | all-gather | bytes 147456 | tf_op jit(solution)/shard_map/all_gather | solution.py:80
  56.2 0.1 fusion.65
  56.3 47.5 %all-gather.5.cloned.1.call-done = f32[32,32,384]{2,1,0:T(8,128)} async-done(((f32[1,32,384]{2,1,0:T(8,128)}), f32[32,32,384]{2,1,0:T(8,128)}) %all-gather.5.cloned.1.call-update) | async-done | bytes 1572880 | tf_op jit(solution)/shard_map/all_gather | solution.py:22
  103.9 1.1 slice.40
  105.0 0.2 fusion.79
  105.2 0.3 fusion.52
  105.4 0.3 fusion.48
  105.7 0.3 fusion.44
  105.9 0.3 fusion.40
  106.2 0.3 fusion.36
  106.5 0.3 fusion.32
  106.7 1.3 slice.41
  108.1 0.4 convolution_select_fusion.5
  108.5 0.4 fusion.28
  108.9 0.4 fusion.27
  109.3 0.4 fusion.26
  109.8 0.4 fusion.25
  110.2 1.1 fusion.24
  111.3 0.0 all-gather.7.cloned.1.call-update
  111.4 4.9 %collective-permute-start = (f32[1024,128]{1,0:T(8,128)S(1)}, f32[1024,128]{1,0:T(8,128)S(1)}, u32[]{:S(2)}, u32[]{:S(2)}) collective-permute-start(f32[1024,128]{1,0:T(8,128)S(1)} %copy-done.2), channel_id=1, source_target_pairs={{1,0},{2,1},{3,2},{4,3},{5,4},{6,5},{7,6},{8,7},{9,8},{10,9},{11,1... | collective-permute-start | bytes 1572872 | tf_op jit(solution)/shard_map/ppermute | solution.py:37
  116.3 3.1 %collective-permute-start.1 = (f32[1024,256]{1,0:T(8,128)S(1)}, f32[1024,256]{1,0:T(8,128)}, u32[]{:S(2)}, u32[]{:S(2)}) collective-permute-start(f32[1024,256]{1,0:T(8,128)S(1)} %gather_fusion), channel_id=1, source_target_pairs={{1,0},{2,1},{3,2},{4,3},{5,4},{6,5},{7,6},{8,7},{9,8},{10,9},{11,1... | collective-permute-start | bytes 3145736 | tf_op jit(solution)/shard_map/ppermute | solution.py:37
  120.1 0.2 multiply_reduce_fusion.1
  120.3 3.5 %fusion.117 = f32[1024,1024]{1,0:T(8,128)S(1)} fusion(f32[1024,128]{1,0:T(8,128)S(1)} %copy-done.2), kind=kOutput, calls=%fused_computation.148 | convolution fusion | flops 1610612736 | bytes 4718592 | tf_op jit(solution)/shard_map/dot_general | solution.py:53
  123.8 4.8 %collective-permute-done = f32[1024,128]{1,0:T(8,128)S(1)} collective-permute-done((f32[1024,128]{1,0:T(8,128)S(1)}, f32[1024,128]{1,0:T(8,128)S(1)}, u32[]{:S(2)}, u32[]{:S(2)}) %collective-permute-start) | collective-permute-done | bytes 524320 | tf_op jit(solution)/shard_map/ppermute | solution.py:37
  128.5 0.2 multiply_reduce_fusion
  128.8 3.5 %fusion.118 = f32[1024,1024]{1,0:T(8,128)S(1)} fusion(f32[1024,128]{1,0:T(8,128)S(1)} %copy-done.2, f32[1024,128]{1,0:T(8,128)S(1)} %collective-permute-done), kind=kOutput, calls=%fused_computation.149 | convolution fusion | flops 1610612736 | bytes 5242880 | tf_op jit(solution)/shard_map/dot_general | solution.py:53
  132.3 1.9 %copy-done.1 = f32[1024,1024]{1,0:T(8,128)} copy-done((f32[1024,1024]{1,0:T(8,128)}, f32[1024,1024]{1,0:T(8,128)S(1)}, u32[]{:S(2)}) %copy-start.1) | copy-done | bytes 4194328
  134.2 8.3 %fusion.6 = f32[1024,256]{1,0:T(8,128)} fusion(f32[1024,256]{1,0:T(8,128)S(1)} %gather_fusion, f32[1024,1024]{1,0:T(8,128)S(1)} %fusion.118, f32[1024]{0:T(1024)S(1)} %multiply_reduce_fusion, f32[1024]{0:T(1024)S(1)} %multiply_reduce_fusion.1), kind=kOutput, calls=%fused_computation.9 | convolution fusion | flops 3225419776 | bytes 6299648 | tf_op jit(solution)/shard_map/dot_general | solution.py:47
  142.5 2.7 %collective-permute-start.2 = (f32[1024,256]{1,0:T(8,128)}, f32[1024,256]{1,0:T(8,128)}, u32[]{:S(2)}, u32[]{:S(2)}) collective-permute-start(f32[1024,256]{1,0:T(8,128)} %fusion.6), channel_id=1, source_target_pairs={{0,1},{1,2},{2,3},{3,4},{4,5},{5,6},{6,7},{7,8},{8,9},{9,10},{10,1... | collective-permute-start | bytes 3145736 | tf_op jit(solution)/shard_map/ppermute | solution.py:37
  145.2 0.7 fusion.109
  145.9 5.0 %fusion = f32[1024,256]{1,0:T(8,128)} fusion(f32[1024,256]{1,0:T(8,128)S(1)} %gather_fusion, f32[1024,1024]{1,0:T(8,128)S(1)} %fusion.117, f32[1024]{0:T(1024)S(1)} %multiply_reduce_fusion.1), kind=kOutput, calls=%fused_computation.3 | convolution fusion | flops 3225419776 | bytes 6295552 | tf_op jit(solution)/shard_map/dot_general | solution.py:41
  150.9 1.8 reduce_sum.113
  152.7 0.6 fusion.55
  153.3 1.0 convolution_bitcast_fusion
  154.3 7.9 %collective-permute-done.2 = f32[1024,256]{1,0:T(8,128)} collective-permute-done((f32[1024,256]{1,0:T(8,128)}, f32[1024,256]{1,0:T(8,128)}, u32[]{:S(2)}, u32[]{:S(2)}) %collective-permute-start.2) | collective-permute-done | bytes 1048608 | tf_op jit(solution)/shard_map/ppermute | solution.py:37
  162.2 8.2 %fusion.23 = f32[1024,256]{1,0:T(8,128)S(1)} fusion(f32[1024,256]{1,0:T(8,128)S(1)} %convolution_bitcast_fusion, f32[1024,256]{1,0:T(8,128)} %fusion, f32[1024,256]{1,0:T(8,128)} %collective-permute-done.1, f32[1024,1024]{1,0:T(8,128)} %copy-done.1, f32[1024]{0:T(1024)S(1)} %multiply_reduce_fusion, f32[1024]{0:T(1024)S(1)} %multiply_reduce_fusion.1, ...), kind=kOutput, calls=%fused_computation.27 | convolution fusion | flops 3226730496 | bytes 9445378 | tf_op jit(solution)/shard_map/dot_general | solution.py:41
  170.4 5.8 %scatter_custom_fusion = f32[1024,256]{1,0:T(8,128)} fusion(s32[1024]{0:T(1024)S(1)} %get-tuple-element.20, f32[1024,256]{1,0:T(8,128)S(1)} %fusion.23, f32[]{:T(128)} %constant.18.clone.1), kind=kCustom, calls=%fused_computation.71 | custom fusion | bytes 1048580 | tf_op jit(solution)/shard_map/scatter | solution.py:97
  (19 shorter events, 0.1 us)
Async XLA Ops:
  6.5 5.5 %copy-start = (f32[1024,256]{1,0:T(8,128)S(1)}, f32[1024,256]{1,0:T(8,128)}, u32[]{:S(2)}) copy-start(f32[1024,256]{1,0:T(8,128)} %param.13) | copy-start | bytes 3145732
  6.5 97.4 %all-gather.5.cloned.1.call-start = ((), (), s32[]{:S(2)}) async-start(), calls=%async_computation.1 | async-start | bytes 1622016 | tf_op jit(solution)/shard_map/all_gather | solution.py:22
  7.3 6.6 %copy-start.3 = (f32[1,256,256]{2,1,0:T(8,128)S(1)}, f32[1,256,256]{2,1,0:T(8,128)}, u32[]{:S(2)}) copy-start(f32[1,256,256]{2,1,0:T(8,128)} %param.14) | copy-start | bytes 786436
  7.3 19.0 %copy-start.4 = (f32[1,32,128]{2,1,0:T(8,128)S(1)}, f32[1,32,128]{2,1,0:T(8,128)}, u32[]{:S(2)}) copy-start(f32[1,32,128]{2,1,0:T(8,128)} %param.15) | copy-start | bytes 49156
  7.3 19.7 %copy-start.5 = (s32[32,6]{0,1:T(8,128)S(1)}, s32[32,6]{0,1:T(8,128)}, u32[]{:S(2)}) copy-start(s32[32,6]{0,1:T(8,128)} %param.16) | copy-start | bytes 2308
  7.3 27.9 %copy-start.7 = (s32[32]{0:T(128)S(1)}, s32[32]{0:T(128)}, u32[]{:S(2)}) copy-start(s32[32]{0:T(128)} %param.17) | copy-start | bytes 388
  27.0 84.4 %copy-start.2 = (f32[1024,128]{1,0:T(8,128)S(1)}, f32[1024,128]{1,0:T(8,128)}, u32[]{:S(2)}) copy-start(f32[1024,128]{1,0:T(8,128)} %param.11) | copy-start | bytes 1572868
  27.0 123.9 %all-gather.7.cloned.1.call-start = ((), (), s32[]{:S(2)}) async-start(), calls=%async_computation.2 | async-start | bytes 2359296 | tf_op jit(solution)/shard_map/all_gather | solution.py:30
  111.4 17.2 %collective-permute-start = (f32[1024,128]{1,0:T(8,128)S(1)}, f32[1024,128]{1,0:T(8,128)S(1)}, u32[]{:S(2)}, u32[]{:S(2)}) collective-permute-start(f32[1024,128]{1,0:T(8,128)S(1)} %copy-done.2), channel_id=1, source_target_pairs={{1,0},{2,1},{3,2},{4,3},{5,4},{6,5},{7,6},{8,7},{9,8},{10,9},{11,1... | collective-permute-start | bytes 1572872 | tf_op jit(solution)/shard_map/ppermute | solution.py:37
  116.3 38.1 %collective-permute-start.1 = (f32[1024,256]{1,0:T(8,128)S(1)}, f32[1024,256]{1,0:T(8,128)}, u32[]{:S(2)}, u32[]{:S(2)}) collective-permute-start(f32[1024,256]{1,0:T(8,128)S(1)} %gather_fusion), channel_id=1, source_target_pairs={{1,0},{2,1},{3,2},{4,3},{5,4},{6,5},{7,6},{8,7},{9,8},{10,9},{11,1... | collective-permute-start | bytes 3145736 | tf_op jit(solution)/shard_map/ppermute | solution.py:37
  132.3 1.9 %copy-start.1 = (f32[1024,1024]{1,0:T(8,128)}, f32[1024,1024]{1,0:T(8,128)S(1)}, u32[]{:S(2)}) copy-start(f32[1024,1024]{1,0:T(8,128)S(1)} %fusion.118) | copy-start | bytes 12582916
  134.2 11.0 %copy-start.6 = (s32[1,2]{1,0:T(1,128)S(1)}, s32[1,2]{1,0:T(1,128)}, u32[]{:S(2)}) copy-start(s32[1,2]{1,0:T(1,128)} %param.18) | copy-start | bytes 28
  142.5 19.7 %collective-permute-start.2 = (f32[1024,256]{1,0:T(8,128)}, f32[1024,256]{1,0:T(8,128)}, u32[]{:S(2)}, u32[]{:S(2)}) collective-permute-start(f32[1024,256]{1,0:T(8,128)} %fusion.6), channel_id=1, source_target_pairs={{0,1},{1,2},{2,3},{3,4},{4,5},{5,6},{6,7},{7,8},{8,9},{9,10},{10,1... | collective-permute-start | bytes 3145736 | tf_op jit(solution)/shard_map/ppermute | solution.py:37
Sparse Core Ops, SparseCore 0:
  27.1 76.7 all-gather.4
  111.5 26.4 all-gather.6
where the time goes:
time: 184 us; the launch traced here: 183 us
  waiting for transfers between devices  60.2 us (33%)
  matrix products  37.2 us (20%)
  between operations  29.5 us (16%)
  blocking collectives  24.5 us (13%)
  local copies, waits for them, and re-layouts  16.2 us (9%)
  starting transfers between devices  10.8 us (6%)
  other arithmetic  4.62 us (3%)
    all_gather x1, waiting for transfers between devices, side_by_side(): lax.all_gather(both, axis, axis=dim, tiled=True)  47.5 us
    dot_general x10, matrix products, multiply(): lax.dot_general(left, right, (((1,), (0,)), ((), ())), precision=HIGH, pr...  18 us
    all_gather x1, blocking collectives, shards(): skel_full = lax.all_gather(skeleton[0], 'leaf', axis=0, tiled=True)  12.8 us
    ppermute x3, waiting for transfers between devices, passed_along(): return lax.ppermute(block, axis, route)  12.7 us
    all_to_all x1, blocking collectives, sent_and_summed(): blocks = lax.all_to_all(split_up(x, dim, size), axis, 0, 0, tiled=True)  11.8 us
    dot_general x3, matrix products, multiply_first(): lax.dot_general(left, right, (((0,), (0,)), ((), ())), precision=HIGH, pr...  10.7 us
    ppermute x3, starting transfers between devices, passed_along(): return lax.ppermute(block, axis, route)  10.7 us
    dot_general x8, matrix products, kernel_tile(): lax.dot_general(left, right, (((1,), (1,)), ((), ())), precision=HIGH, pr...  8.51 us
  transfers between devices with their start and end apart: 5, of which 3 were waited for; matrix products, arithmetic and copies ran while one was open for 14% of the time, Pallas kernels for 0%

commit v1 on v0

v1 whole, which is shorter than its diff:
```python
import jax
import jax.numpy as jnp
from jax import lax
from jax.experimental import pallas as pl
from jax.experimental.pallas import tpu as pltpu
from jax.sharding import PartitionSpec as P

MESH = pl.DeviceIdType.MESH
F32, BF16 = jnp.float32, jnp.bfloat16
LEAVES, WIDE, NX, NZ = 8, 32, 4, 8
ROWS, FEAT, RANK, COLS = 1024, 128, 256, 256
FAR, PART = 6, 32
BLOCK = 256
STEPS = ROWS // BLOCK
RHS_CHUNK = 128
COPIES = 96
SCALE = -(2.0 / FEAT) * 1.4426950408889634

LAST = (((1,), (1,)), ((), ()))
FIRST = (((0,), (0,)), ((), ()))
PLAIN = (((1,), (0,)), ((), ()))


def dot(a, b, dims=PLAIN):
    return lax.dot_general(a, b, dims, preferred_element_type=F32)


def split(x):
    high = x.astype(BF16)
    return high, (x - high.astype(F32)).astype(BF16)


def dot3(a, b, dims=PLAIN):
    return dot(a[0], b[0], dims) + (dot(a[0], b[1], dims) + dot(a[1], b[0], dims))


def kernel(
    order, far_ids, far_count, near_ids, near_count, rhs, points, basis, transfer, skeleton, out,
    moved, q, own_hl, own_lh, own_col, own_row, q_in, in_hl, in_lh, in_col, in_row,
    basis_h, basis_l, rhs_h, rhs_l, rhs_in, in_h, in_l, share_out, share_in,
    lifted, pieces, coefs, skel_parent, skels, chosen_out, chosen, tile_h, tile_l, field,
    send_sems, recv_sems,
):
    leaf, wide = lax.axis_index("leaf"), lax.axis_index("wide")
    x, z = lax.div(wide, NZ), lax.rem(wide, NZ)
    step = 2 * lax.rem(leaf, 2) - 1
    ahead, behind = lax.rem(wide + step + WIDE, WIDE), lax.rem(wide - step + WIDE, WIDE)

    def leaf_peer(d):
        return lax.rem(leaf + d, LEAVES), wide

    def z_peer(d):
        return leaf, x * NZ + lax.rem(z + d, NZ)

    def x_peer(d):
        return leaf, lax.rem(x + d, NX) * NZ + z

    barrier = pltpu.get_barrier_semaphore()
    partners = [leaf_peer(d) for d in range(1, LEAVES)] + [z_peer(d) for d in range(1, NZ)]
    partners += [x_peer(d) for d in range(1, NX)] + [(leaf, ahead), (leaf, behind)]
    for partner in partners:
        pl.semaphore_signal(barrier, inc=1, device_id=partner, device_id_type=MESH)
    pl.semaphore_wait(barrier, len(partners))

    copies = []

    def send(src, dst, partner):
        k = len(copies)
        copy = pltpu.make_async_remote_copy(
            src_ref=src, dst_ref=dst, send_sem=send_sems.at[k], recv_sem=recv_sems.at[k],
            device_id=partner, device_id_type=MESH)
        copy.start()
        copies.append(copy)
        return copy

    skel_leaf = [send(skeleton.at[0], skel_parent.at[leaf], leaf_peer(d)) for d in range(1, LEAVES)]
    skel_z = [send(skeleton.at[0], skels.at[wide], z_peer(d)) for d in range(1, NZ)]
    skel_parent[leaf] = skeleton[0]
    skels[wide] = skeleton[0]

    def send_rhs(first, last):
        return [
            send(rhs.at[pl.ds(i * RHS_CHUNK, RHS_CHUNK)], rhs_in.at[pl.ds(i * RHS_CHUNK, RHS_CHUNK)], (leaf, ahead))
            for i in range(first, last)]

    near_rhs = send_rhs(0, 2)

    moved[:, 0:128], moved[:, 128:256] = split(points[...])
    moved[:, 256:512], moved[:, 512:768] = split(basis[...])
    rhs_h[...], rhs_l[...] = split(rhs[...])

    def reorder(i, carry):
        rows = pl.ds(pl.multiple_of(i * BLOCK, BLOCK), BLOCK)
        place = lax.broadcasted_iota(jnp.int32, (BLOCK, ROWS), 0) + i * BLOCK
        chosen_rows = jnp.where(order[...] == place, 1.0, 0.0).astype(BF16)
        got = dot(chosen_rows, moved[...])
        high, low = got[:, 0:128], got[:, 128:256]
        q[rows, :] = high + low
        own_hl[rows, 0:128] = high.astype(BF16)
        own_hl[rows, 128:256] = low.astype(BF16)
        own_lh[rows, 0:128] = low.astype(BF16)
        own_lh[rows, 128:256] = high.astype(BF16)
        basis_h[rows, :] = got[:, 256:512].astype(BF16)
        basis_l[rows, :] = got[:, 512:768].astype(BF16)
        return carry

    lax.fori_loop(0, STEPS, reorder, 0)
    near_q = [
        send(q.at[pl.ds(i * BLOCK, BLOCK)], q_in.at[pl.ds(i * BLOCK, BLOCK)], (leaf, ahead)) for i in range(STEPS)]
    near_rhs += send_rhs(2, 4)

    basis_hl = (basis_h[...], basis_l[...])
    leaf_coef = dot3((rhs_h[...], rhs_l[...]), basis_hl, FIRST)
    transfer_hl = split(transfer[0])
    lifted[...] = dot3(split(leaf_coef), transfer_hl)
    piece = [
        send(lifted.at[pl.ds(pl.multiple_of(leaf_peer(d)[0] * PART, PART), PART)], pieces.at[leaf], leaf_peer(d))
        for d in range(1, LEAVES)]
    pieces[leaf] = lifted[pl.ds(pl.multiple_of(leaf * PART, PART), PART), :]

    for copy in skel_z:
        copy.wait_recv()
    rows_of_x = pl.ds(x * NZ, NZ)
    skel_x = [send(skels.at[rows_of_x], skels.at[rows_of_x], x_peer(d)) for d in range(1, NX)]

    def norms(points_ref, column, row):
        sq = SCALE * jnp.sum(points_ref[...] * points_ref[...], axis=1, keepdims=True)
        column[...] = sq
        row[...] = jnp.transpose(jnp.broadcast_to(sq, (sq.shape[0], 128)))[0:1, :]

    def tile(left, left_col, right_hl, right_lh, right_row):
        cross = dot(left, right_hl, LAST) + dot(left, right_lh, LAST)
        return split(jnp.exp2((left_col + right_row) - (2.0 * SCALE) * cross))

    norms(q, own_col, own_row)

    def own_term(i, carry):
        rows = pl.ds(pl.multiple_of(i * BLOCK, BLOCK), BLOCK)
        t = tile(own_hl[rows, :], own_col[rows, :], own_hl[...], own_lh[...], own_row[...])
        out[rows, :] = dot3(t, (rhs_h[...], rhs_l[...]))
        return carry

    lax.fori_loop(0, STEPS, own_term, 0)

    for copy in piece:
        copy.wait_recv()
    coefs[wide] = jnp.sum(pieces[...], axis=0)
    coef_z = [send(coefs.at[wide], coefs.at[wide], z_peer(d)) for d in range(1, NZ)]
    coef_x = [send(coefs.at[wide], coefs.at[wide], x_peer(d)) for d in range(1, NX)]
    near_rhs += send_rhs(4, 8)

    for copy in skel_x:
        copy.wait_recv()
    for j in range(FAR):
        chosen_out[j] = skels[far_ids[wide, j]]
    chosen[:, leaf] = chosen_out[...]
    picked = [send(chosen_out, chosen.at[:, leaf], leaf_peer(d)) for d in range(1, LEAVES)]

    for copy in near_q:
        copy.wait_recv()
    high, low = split(q_in[...])
    in_hl[:, 0:128], in_hl[:, 128:256] = high, low
    in_lh[:, 0:128], in_lh[:, 128:256] = low, high
    norms(q_in, in_col, in_row)
    shares = []
    for i in range(STEPS):
        rows = pl.ds(i * BLOCK, BLOCK)
        t = tile(in_hl[rows, :], in_col[rows, :], own_hl[...], own_lh[...], own_row[...])
        share_out[rows, :] = dot3(t, (rhs_h[...], rhs_l[...]))
        shares.append(send(share_out.at[rows], share_in.at[rows], (leaf, behind)))
        for d in ((1, 7), (2, 6), (3, 5), (4,))[i]:
            coef_z[d - 1].wait_recv()
            block = coefs.at[x * NZ + lax.rem(z - d + NZ, NZ)]
            coef_x += [send(block, block, x_peer(e)) for e in range(1, NX)]

    first_id, second_id, used = near_ids[0, 0], near_ids[0, 1], near_count[0]
    number = leaf * WIDE + wide

    def listed(other):
        return jnp.where(((first_id == other) & (used > 0)) | ((second_id == other) & (used > 1)), 1.0, 0.0).astype(F32)

    behind_used, ahead_used = listed(number - step), listed(number + step)

    for copy in near_rhs:
        copy.wait_recv()
    in_h[...], in_l[...] = split(rhs_in[...])

    def near_term(i, carry):
        rows = pl.ds(pl.multiple_of(i * BLOCK, BLOCK), BLOCK)
        t = tile(own_hl[rows, :], own_col[rows, :], in_hl[...], in_lh[...], in_row[...])
        out[rows, :] += behind_used * dot3(t, (in_h[...], in_l[...]))
        return carry

    lax.fori_loop(0, STEPS, near_term, 0)

    for copy in picked + skel_leaf:
        copy.wait_recv()
    targets = skel_parent[...].reshape(RANK, FEAT)
    target_high, target_low = split(targets)
    target_hl = jnp.concatenate([target_high, target_low], axis=1)
    target_lh = jnp.concatenate([target_low, target_high], axis=1)
    target_sq = SCALE * jnp.sum(targets * targets, axis=1, keepdims=True)
    target_row = jnp.transpose(jnp.broadcast_to(target_sq, (RANK, 128)))[0:1, :]
    for j in range(FAR):
        sources = chosen[j].reshape(RANK, FEAT)
        source_sq = SCALE * jnp.sum(sources * sources, axis=1, keepdims=True)
        tile_h[j], tile_l[j] = tile(
            jnp.concatenate(split(sources), axis=1), source_sq, target_hl, target_lh, target_row)

    for copy in coef_x:
        copy.wait_recv()
    total = jnp.zeros((PART, RANK), F32)
    for j in range(FAR):
        mask = jnp.where(far_count[wide] > j, 1.0, 0.0).astype(F32)
        total += mask * dot3(split(coefs[far_ids[wide, j]]), (tile_h[j], tile_l[j]))
    field[leaf] = total
    fields = [send(field.at[leaf], field.at[leaf], leaf_peer(d)) for d in range(1, LEAVES)]
    for copy in fields:
        copy.wait_recv()
    leaf_field = dot3(split(field[...].reshape(COLS, RANK)), transfer_hl, LAST)
    far_out = dot3((basis_h[...], basis_l[...]), split(leaf_field), LAST)

    for copy in shares:
        copy.wait_recv()
    out[...] += far_out + ahead_used * share_in[...]
    for copy in copies:
        copy.wait_send()


def shards(rhs, points, order, basis, transfer, skeleton, far_ids, far_count, near_ids, near_count):
    vmem, smem = pl.BlockSpec(memory_space=pltpu.VMEM), pl.BlockSpec(memory_space=pltpu.SMEM)

    def held(*shape, dtype=F32):
        return pltpu.VMEM(shape, dtype)

    wide_bf16 = held(ROWS, 256, dtype=BF16)
    return pl.pallas_call(
        kernel,
        out_shape=jax.ShapeDtypeStruct((ROWS, COLS), F32),
        in_specs=[vmem, smem, smem, smem, smem] + [vmem] * 5,
        out_specs=vmem,
        scratch_shapes=[
            held(ROWS, 768, dtype=BF16),
            held(ROWS, FEAT), wide_bf16, wide_bf16, held(ROWS, 1), held(1, ROWS),
            held(ROWS, FEAT), wide_bf16, wide_bf16, held(ROWS, 1), held(1, ROWS),
            wide_bf16, wide_bf16, wide_bf16, wide_bf16,
            held(ROWS, COLS), wide_bf16, wide_bf16,
            held(ROWS, COLS), held(ROWS, COLS),
            held(COLS, RANK), held(LEAVES, PART, RANK), held(WIDE, PART, RANK),
            held(LEAVES, PART, FEAT), held(WIDE, PART, FEAT),
            held(FAR, PART, FEAT), held(FAR, LEAVES, PART, FEAT),
            held(FAR, RANK, RANK, dtype=BF16), held(FAR, RANK, RANK, dtype=BF16),
            held(LEAVES, PART, RANK),
            pltpu.SemaphoreType.DMA((COPIES,)),
            pltpu.SemaphoreType.DMA((COPIES,)),
        ],
        compiler_params=pltpu.CompilerParams(
            collective_id=0, has_side_effects=True, vmem_limit_bytes=56 * 1024 * 1024),
    )(order.reshape(1, ROWS), far_ids, far_count, near_ids, near_count, rhs, points, basis, transfer, skeleton)


def solution(mesh):
    placed = (
        P(("leaf", "wide"), None),
        P(("leaf", "wide"), None),
        P(("leaf", "wide")),
        P(("leaf", "wide"), None),
        P(("leaf", "wide"), None, None),
        P("wide", "leaf", None),
        P(),
        P(),
        P(("leaf", "wide"), None),
        P(("leaf", "wide")),
    )
    return jax.shard_map(
        shards, mesh=mesh, in_specs=placed, out_specs=P(("leaf", "wide"), None), check_vma=False
    )
```

time: 184 us -> 76.6 us (0.42)
  the two profiles are of different devices: /device:TPU:2 before, /device:TPU:1 now
where the time goes in v1:
time: 76.6 us; the launch traced here: 76.4 us
  Pallas kernels  72.2 us (94%)
  local copies, waits for them, and re-layouts  3.63 us (5%)
    pallas_call x1, Pallas kernels, shards(): pl.pallas_call(kernel, out_shape=jax.ShapeDtypeStruct((ROWS, COLS), F32),...  72.2 us
    unnamed x2, local copies, waits for them, and re-layouts  3.63 us

profile of v1, /device:TPU:1, one launch (start us, length us, event | category | flops | bytes accessed | tf_op | source)
XLA Modules:
  0.0 76.4 jit_solution(9811233194671911945)
XLA Ops:
  0.7 1.4 %copy.11.far_ids = s32[32,6]{1,0:T(8,128)} copy(s32[32,6]{0,1:T(8,128)} %param.16) | data formatting | bytes 1536 | tf_op args[6]
  2.0 72.2 %shard_map.100 = f32[1024,256]{1,0:T(8,128)} custom-call(s32[1,1024]{1,0:T(1,128)} %bitcast.1, s32[32,6]{1,0:T(8,128)} %copy.11.far_ids, s32[32]{0:T(128)} %far_count.1, s32[1,2]{1,0:T(1,128)} %near_ids.1, s32[1]{0:T(128)S(6)} %copy.13.near_count, f32[1024,256]{1,0:T(8,128)} %rhs.1, f32[1024,128]{1,0:T(8,128)} %points.1, f32[1024,256]{1,0:T(8,128)} %basis.1, ...), custom_call_target="tpu_custom_call" | custom-call | tf_op jit(solution)/shard_map/pallas_call | solution.py:237
  74.2 2.3 %copy.14 = f32[1024,256]{1,0:T(8,128)} copy(f32[1024,256]{1,0:T(8,128)} %shard_map.100) | data formatting | bytes 2097152

commit v2 on v1

v2 whole, which is shorter than its diff:
```python
import jax
import jax.numpy as jnp
from jax import lax
from jax.experimental import pallas as pl
from jax.experimental.pallas import tpu as pltpu
from jax.sharding import PartitionSpec as P

MESH = pl.DeviceIdType.MESH
F32, BF16 = jnp.float32, jnp.bfloat16
LEAVES, WIDE, NX, NZ = 8, 32, 4, 8
ROWS, FEAT, RANK, COLS = 1024, 128, 256, 256
FAR, PART = 6, 32
BLOCK = 256
STEPS = ROWS // BLOCK
RHS_CHUNK = 128
COPIES = 128
SCALE = -(2.0 / FEAT) * 1.4426950408889634

LAST = (((1,), (1,)), ((), ()))
FIRST = (((0,), (0,)), ((), ()))
PLAIN = (((1,), (0,)), ((), ()))


def dot(a, b, dims=PLAIN):
    return lax.dot_general(a, b, dims, preferred_element_type=F32)


def split(x):
    high = x.astype(BF16)
    return high, (x - high.astype(F32)).astype(BF16)


def dot3(a, b, dims=PLAIN):
    return dot(a[0], b[0], dims) + (dot(a[0], b[1], dims) + dot(a[1], b[0], dims))


def kernel(
    order, far_ids, far_count, near_ids, near_count, rhs_hbm, points_hbm, basis_hbm, transfer_hbm, skeleton,
    out, share,
    rhs, points, basis, transfer,
    moved, q, own_hl, own_lh, own_col, own_row, q_in, in_hl, in_lh, in_col, in_row,
    basis_h, basis_l, rhs_h, rhs_l, rhs_in, in_h, in_l, share_out, share_in,
    lifted, half, pieces, coefs, skel_parent, skels, chosen, tile_h, tile_l, field,
    load_sems, send_sems, recv_sems,
):
    leaf, wide = lax.axis_index("leaf"), lax.axis_index("wide")
    core, chip = lax.rem(leaf, 2), lax.div(leaf, 2)
    x, z = lax.div(wide, NZ), lax.rem(wide, NZ)
    step = 2 * core - 1
    ahead, behind = lax.rem(wide + step + WIDE, WIDE), lax.rem(wide - step + WIDE, WIDE)
    way = 2 * lax.div(z, NZ - 1) - 1

    def leaf_peer(d):
        return lax.rem(leaf + d, LEAVES), wide

    def z_index(d):
        return x * NZ + lax.rem(z + d + NZ, NZ)

    def x_index(d):
        return lax.rem(x + d + 3 * NX, NX) * NZ

    loads = []
    for source, target in ((rhs_hbm, rhs), (points_hbm, points), (basis_hbm, basis), (transfer_hbm, transfer)):
        load = pltpu.make_async_copy(source, target, load_sems.at[len(loads)])
        load.start()
        loads.append(load)

    barrier = pltpu.get_barrier_semaphore()
    partners = [leaf_peer(d) for d in range(1, LEAVES)] + [(leaf, z_index(d)) for d in range(1, NZ)]
    partners += [(leaf, x_index(1) + z), (leaf, x_index(-1) + z), (leaf, ahead), (leaf, behind)]
    for partner in partners:
        pl.semaphore_signal(barrier, inc=1, device_id=partner, device_id_type=MESH)
    pl.semaphore_wait(barrier, len(partners))

    copies = []

    def send(src, dst, partner):
        k = len(copies)
        copy = pltpu.make_async_remote_copy(
            src_ref=src, dst_ref=dst, send_sem=send_sems.at[k], recv_sem=recv_sems.at[k],
            device_id=partner, device_id_type=MESH)
        copy.start()
        copies.append(copy)
        return copy

    def arrived(group):
        for copy in group:
            copy.wait_recv()

    FARTHEST_FIRST = (4, 3, -3, 2, -2, 1, -1)

    def along_z(buffer):
        block = buffer.at[wide]
        return {d: send(block, block, (leaf, z_index(d))) for d in FARTHEST_FIRST}

    def to_x_neighbours(blocks):
        return [send(blocks, blocks, (leaf, x_index(d) + z)) for d in (way, -way)]

    def passed_on(sent, blocks):
        sent[0].wait_recv()
        return [sent[1], send(blocks, blocks, (leaf, x_index(way) + z))]

    skels[wide] = skeleton[0]
    skel_z = list(along_z(skels).values())
    skel_leaf = [send(skeleton.at[0], skel_parent.at[leaf], leaf_peer(d)) for d in range(1, LEAVES)]
    skel_parent[leaf] = skeleton[0]

    near_rhs, near_q, shares = [], [], []

    def send_rhs(count):
        for _ in range(count):
            rows = pl.ds(len(near_rhs) * RHS_CHUNK, RHS_CHUNK)
            near_rhs.append(send(rhs.at[rows], rhs_in.at[rows], (leaf, ahead)))

    loads[0].wait()
    send_rhs(3)
    rhs_h[...], rhs_l[...] = split(rhs[...])
    loads[1].wait()
    loads[2].wait()

    moved[:, 0:128], moved[:, 128:256] = split(points[...])
    moved[:, 256:512], moved[:, 512:768] = split(basis[...])

    def reorder(i, carry):
        rows = pl.ds(pl.multiple_of(i * BLOCK, BLOCK), BLOCK)
        place = lax.broadcasted_iota(jnp.int32, (BLOCK, ROWS), 0) + i * BLOCK
        chosen_rows = jnp.where(order[...] == place, 1.0, 0.0).astype(BF16)
        got = dot(chosen_rows, moved[...])
        high, low = got[:, 0:128], got[:, 128:256]
        q[rows, :] = high + low
        own_hl[rows, 0:128] = high.astype(BF16)
        own_hl[rows, 128:256] = low.astype(BF16)
        own_lh[rows, 0:128] = low.astype(BF16)
        own_lh[rows, 128:256] = high.astype(BF16)
        basis_h[rows, :] = got[:, 256:512].astype(BF16)
        basis_l[rows, :] = got[:, 512:768].astype(BF16)
        return carry

    lax.fori_loop(0, STEPS, reorder, 0)
    for i in range(STEPS):
        rows = pl.ds(i * BLOCK, BLOCK)
        near_q.append(send(q.at[rows], q_in.at[rows], (leaf, ahead)))

    leaf_coef = dot3((rhs_h[...], rhs_l[...]), (basis_h[...], basis_l[...]), FIRST)
    loads[3].wait()
    transfer_hl = split(transfer[0])
    lifted[...] = dot3(split(leaf_coef), transfer_hl).reshape(LEAVES // 2, 2, PART, RANK)
    halved = [send(lifted.at[:, 1 - core], half.at[:, 0], (leaf - step, wide))]

    def norms(points_ref, column, row):
        sq = SCALE * jnp.sum(points_ref[...] * points_ref[...], axis=1, keepdims=True)
        column[...] = sq
        row[...] = jnp.transpose(jnp.broadcast_to(sq, (sq.shape[0], 128)))[0:1, :]

    def tile(left, left_col, right_hl, right_lh, right_row):
        cross = dot(left, right_hl, LAST) + dot(left, right_lh, LAST)
        return split(jnp.exp2((left_col + right_row) - (2.0 * SCALE) * cross))

    def own_term(i, carry):
        rows = pl.ds(pl.multiple_of(i * BLOCK, BLOCK), BLOCK)
        t = tile(own_hl[rows, :], own_col[rows, :], own_hl[...], own_lh[...], own_row[...])
        out[rows, :] = dot3(t, (rhs_h[...], rhs_l[...]))
        return carry

    norms(q, own_col, own_row)
    arrived(halved)
    half[:, 1] = half[:, 0] + lifted[:, core]
    pieces[chip] = half[chip, 1]
    piece = []
    for d in (2, 1, 3):
        other = lax.rem(chip + d, LEAVES // 2)
        piece.append(send(half.at[other, 1], pieces.at[chip], (2 * other + core, wide)))
    own_rows = pl.ds(x * NZ, NZ)
    arrived(skel_z)
    skel_x = to_x_neighbours(skels.at[own_rows])
    lax.fori_loop(0, STEPS, own_term, 0)

    arrived(piece)
    coefs[wide] = jnp.sum(pieces[...], axis=0)
    coef_z = along_z(coefs)
    coef_x = {0: to_x_neighbours(coefs.at[wide])}
    send_rhs(2)
    skel_x = passed_on(skel_x, skels.at[pl.ds(x_index(-way), NZ)])

    def along_x(*offsets):
        for d in offsets:
            coef_z[d].wait_recv()
            coef_x[d] = to_x_neighbours(coefs.at[z_index(-d)])

    def onward(*offsets):
        for d in offsets:
            coef_x[d] = passed_on(coef_x[d], coefs.at[x_index(-way) + lax.rem(z - d + NZ, NZ)])

    arrived(near_q)
    high, low = split(q_in[...])
    in_hl[:, 0:128], in_hl[:, 128:256] = high, low
    in_lh[:, 0:128], in_lh[:, 128:256] = low, high
    norms(q_in, in_col, in_row)

    def share_term(i):
        rows = pl.ds(i * BLOCK, BLOCK)
        t = tile(in_hl[rows, :], in_col[rows, :], own_hl[...], own_lh[...], own_row[...])
        share_out[rows, :] = dot3(t, (rhs_h[...], rhs_l[...]))
        shares.append(send(share_out.at[rows], share_in.at[rows], (leaf, behind)))

    share_term(0)
    along_x(1, -1, 2, -2)
    send_rhs(1)
    share_term(1)
    along_x(3, -3, 4)
    send_rhs(2)
    onward(0)
    share_term(2)
    onward(1, -1, 2, -2)

    arrived(skel_x)
    for j in range(FAR):
        chosen[chip, core, j] = skels[far_ids[j, wide]]
    picked = [send(chosen.at[chip, core], chosen.at[chip, core], leaf_peer(d)) for d in (2, 4, 6)]
    share_term(3)
    onward(3, -3, 4)

    first_id, second_id, used = near_ids[0, 0], near_ids[0, 1], near_count[0]
    number = leaf * WIDE + wide

    def listed(other):
        return jnp.where(((first_id == other) & (used > 0)) | ((second_id == other) & (used > 1)), 1.0, 0.0).astype(F32)

    behind_used, ahead_used = listed(number - step), listed(number + step)

    arrived(near_rhs)
    in_h[...], in_l[...] = split(rhs_in[...])

    def near_term(i, carry):
        rows = pl.ds(pl.multiple_of(i * BLOCK, BLOCK), BLOCK)
        t = tile(own_hl[rows, :], own_col[rows, :], in_hl[...], in_lh[...], in_row[...])
        out[rows, :] += behind_used * dot3(t, (in_h[...], in_l[...]))
        return carry

    lax.fori_loop(0, 2, near_term, 0)
    arrived(picked)
    picked = [send(chosen.at[:, core], chosen.at[:, core], (leaf - step, wide))]
    lax.fori_loop(2, STEPS, near_term, 0)

    arrived(picked + skel_leaf)
    targets = skel_parent[...].reshape(RANK, FEAT)
    target_high, target_low = split(targets)
    target_hl = jnp.concatenate([target_high, target_low], axis=1)
    target_lh = jnp.concatenate([target_low, target_high], axis=1)
    target_sq = SCALE * jnp.sum(targets * targets, axis=1, keepdims=True)
    target_row = jnp.transpose(jnp.broadcast_to(target_sq, (RANK, 128)))[0:1, :]
    for j in range(FAR):
        sources = chosen[:, :, j].reshape(RANK, FEAT)
        source_sq = SCALE * jnp.sum(sources * sources, axis=1, keepdims=True)
        tile_h[j], tile_l[j] = tile(
            jnp.concatenate(split(sources), axis=1), source_sq, target_hl, target_lh, target_row)

    for group in coef_x.values():
        arrived(group)
    total = jnp.zeros((PART, RANK), F32)
    for j in range(FAR):
        mask = jnp.where(far_count[wide] > j, 1.0, 0.0).astype(F32)
        total += mask * dot3(split(coefs[far_ids[j, wide]]), (tile_h[j], tile_l[j]))
    field[chip, core] = total
    partner = (leaf - step, wide)
    fields = [send(field.at[chip, core], field.at[chip, core], leaf_peer(d)) for d in (4, 2, 6)]
    inside = [send(field.at[chip, core], field.at[chip, core], partner)]
    arrived(shares)
    share[...] = ahead_used * share_in[...]
    for copy, d in ((fields[1], 2), (fields[2], 6), (fields[0], 4)):
        copy.wait_recv()
        block = field.at[lax.rem(chip + LEAVES // 2 - d // 2, LEAVES // 2), core]
        inside.append(send(block, block, partner))
    arrived(inside)
    leaf_field = dot3(split(field[...].reshape(COLS, RANK)), transfer_hl, LAST)
    out[...] += dot3((basis_h[...], basis_l[...]), split(leaf_field), LAST)
    for copy in copies:
        copy.wait_send()


def shards(rhs, points, order, basis, transfer, skeleton, far_ids, far_count, near_ids, near_count):
    vmem, smem, anywhere = (pl.BlockSpec(memory_space=m) for m in (pltpu.VMEM, pltpu.SMEM, pl.ANY))

    def held(*shape, dtype=F32):
        return pltpu.VMEM(shape, dtype)

    wide_bf16 = held(ROWS, 256, dtype=BF16)
    total, share = pl.pallas_call(
        kernel,
        out_shape=(jax.ShapeDtypeStruct((ROWS, COLS), F32), jax.ShapeDtypeStruct((ROWS, COLS), F32)),
        in_specs=[vmem, smem, smem, smem, smem] + [anywhere] * 4 + [vmem],
        out_specs=(vmem, vmem),
        scratch_shapes=[
            held(ROWS, COLS), held(ROWS, FEAT), held(ROWS, RANK), held(1, RANK, RANK),
            held(ROWS, 768, dtype=BF16),
            held(ROWS, FEAT), wide_bf16, wide_bf16, held(ROWS, 1), held(1, ROWS),
            held(ROWS, FEAT), wide_bf16, wide_bf16, held(ROWS, 1), held(1, ROWS),
            wide_bf16, wide_bf16, wide_bf16, wide_bf16,
            held(ROWS, COLS), wide_bf16, wide_bf16,
            held(ROWS, COLS), held(ROWS, COLS),
            held(LEAVES // 2, 2, PART, RANK), held(LEAVES // 2, 2, PART, RANK),
            held(LEAVES // 2, PART, RANK), held(WIDE, PART, RANK),
            held(LEAVES, PART, FEAT), held(WIDE, PART, FEAT),
            held(LEAVES // 2, 2, FAR, PART, FEAT),
            held(FAR, RANK, RANK, dtype=BF16), held(FAR, RANK, RANK, dtype=BF16),
            held(LEAVES // 2, 2, PART, RANK),
            pltpu.SemaphoreType.DMA((4,)),
            pltpu.SemaphoreType.DMA((COPIES,)),
            pltpu.SemaphoreType.DMA((COPIES,)),
        ],
        compiler_params=pltpu.CompilerParams(
            collective_id=0, has_side_effects=True, vmem_limit_bytes=56 * 1024 * 1024),
    )(order.reshape(1, ROWS), far_ids.T, far_count, near_ids, near_count, rhs, points, basis, transfer, skeleton)
    return total + share


def solution(mesh):
    placed = (
        P(("leaf", "wide"), None),
        P(("leaf", "wide"), None),
        P(("leaf", "wide")),
        P(("leaf", "wide"), None),
        P(("leaf", "wide"), None, None),
        P("wide", "leaf", None),
        P(),
        P(),
        P(("leaf", "wide"), None),
        P(("leaf", "wide")),
    )
    return jax.shard_map(
        shards, mesh=mesh, in_specs=placed, out_specs=P(("leaf", "wide"), None), check_vma=False
    )
```

time: 76.6 us -> 69.4 us (0.906)
  Pallas kernels: 72.2 us -> 65.9 us
  local copies, waits for them, and re-layouts: 3.63 us -> 0 us
  other arithmetic: 0 us -> 2.65 us
    pallas_call x1, Pallas kernels: 72.2 us -> 65.9 us  [shards(): pl.pallas_call(kernel, out_shape=(jax.ShapeDtypeStruct((ROWS, COLS), F32)...]
    unnamed x2 -> x0, local copies, waits for them, and re-layouts: 3.63 us -> none
    add x0 -> x1, other arithmetic: none -> 2.65 us  [shards(): return total + share]
where the time goes in v2:
time: 69.4 us; the launch traced here: 69.2 us
  Pallas kernels  65.9 us (95%)
  other arithmetic  2.65 us (4%)
    pallas_call x1, Pallas kernels, shards(): pl.pallas_call(kernel, out_shape=(jax.ShapeDtypeStruct((ROWS, COLS), F32)...  65.9 us
    add x1, other arithmetic, shards(): return total + share  2.65 us

profile of v2, /device:TPU:1, one launch (start us, length us, event | category | flops | bytes accessed | tf_op | source)
XLA Modules:
  0.0 69.2 jit_solution(17086120853432123592)
XLA Ops:
  0.7 65.9 %shard_map.100 = (f32[1024,256]{1,0:T(8,128)}, f32[1024,256]{1,0:T(8,128)}) custom-call(s32[1,1024]{1,0:T(1,128)} %bitcast.2, s32[6,32]{1,0:T(8,128)} %bitcast.3, s32[32]{0:T(128)} %far_count.1, s32[1,2]{1,0:T(1,128)} %near_ids.1, s32[1]{0:T(128)S(6)} %copy.11.near_count, f32[1024,256]{1,0:T(8,128)} %rhs_hbm.1, f32[1024,128]{1,0:T(8,128)} %points_hbm.1, ...), custom_call_target="tpu_custom_call" | custom-call | tf_op jit(solution)/shard_map/pallas_call | solution.py:288
  66.6 2.6 %add.3 = f32[1024,256]{1,0:T(8,128)} add(f32[1024,256]{1,0:T(8,128)} %get-tuple-element.7, f32[1024,256]{1,0:T(8,128)} %get-tuple-element.8) | non-fusion elementwise | flops 262144 | bytes 3145728 | tf_op jit(solution)/shard_map/add | solution.py:314

commit v3 on v2

--- a/solution.py
+++ b/solution.py
@@ -19,6 +19,7 @@
 LAST = (((1,), (1,)), ((), ()))
 FIRST = (((0,), (0,)), ((), ()))
 PLAIN = (((1,), (0,)), ((), ()))
+FARTHEST_FIRST = (4, 3, -3, 2, -2, 1, -1)
 
 
 def dot(a, b, dims=PLAIN):
@@ -40,7 +41,8 @@
     rhs, points, basis, transfer,
     moved, q, own_hl, own_lh, own_col, own_row, q_in, in_hl, in_lh, in_col, in_row,
     basis_h, basis_l, rhs_h, rhs_l, rhs_in, in_h, in_l, share_out, share_in,
-    lifted, half, pieces, coefs, skel_parent, skels, chosen, tile_h, tile_l, field,
+    lifted, half, pieces, coefs, skels, far_points, far_hl, far_lh, far_col, far_row, tile_h, tile_l,
+    parts_out, parts_in, field,
     load_sems, send_sems, recv_sems,
 ):
     leaf, wide = lax.axis_index("leaf"), lax.axis_index("wide")
@@ -48,7 +50,6 @@
     x, z = lax.div(wide, NZ), lax.rem(wide, NZ)
     step = 2 * core - 1
     ahead, behind = lax.rem(wide + step + WIDE, WIDE), lax.rem(wide - step + WIDE, WIDE)
-    way = 2 * lax.div(z, NZ - 1) - 1
 
     def leaf_peer(d):
         return lax.rem(leaf + d, LEAVES), wide
@@ -67,7 +68,7 @@
 
     barrier = pltpu.get_barrier_semaphore()
     partners = [leaf_peer(d) for d in range(1, LEAVES)] + [(leaf, z_index(d)) for d in range(1, NZ)]
-    partners += [(leaf, x_index(1) + z), (leaf, x_index(-1) + z), (leaf, ahead), (leaf, behind)]
+    partners += [(leaf, x_index(d) + z) for d in range(1, NX)] + [(leaf, ahead), (leaf, behind)]
     for partner in partners:
         pl.semaphore_signal(barrier, inc=1, device_id=partner, device_id_type=MESH)
     pl.semaphore_wait(barrier, len(partners))
@@ -89,21 +90,12 @@
 
     FARTHEST_FIRST = (4, 3, -3, 2, -2, 1, -1)
 
-    def along_z(buffer):
-        block = buffer.at[wide]
-        return {d: send(block, block, (leaf, z_index(d))) for d in FARTHEST_FIRST}
-
-    def to_x_neighbours(blocks):
-        return [send(blocks, blocks, (leaf, x_index(d) + z)) for d in (way, -way)]
-
-    def passed_on(sent, blocks):
-        sent[0].wait_recv()
-        return [sent[1], send(blocks, blocks, (leaf, x_index(way) + z))]
-
-    skels[wide] = skeleton[0]
-    skel_z = list(along_z(skels).values())
-    skel_leaf = [send(skeleton.at[0], skel_parent.at[leaf], leaf_peer(d)) for d in range(1, LEAVES)]
-    skel_parent[leaf] = skeleton[0]
+    own_set = skels.at[chip, core]
+    partner = (leaf - step, wide)
+    skel_row = [send(skeleton.at[0], own_set.at[z], (leaf, z_index(d))) for d in FARTHEST_FIRST]
+    skel_row += [send(skeleton.at[0], own_set.at[NZ + x], (leaf, x_index(d) + z)) for d in (2, 1, 3)]
+    skels[chip, core, z] = skeleton[0]
+    skels[chip, core, NZ + x] = skeleton[0]
 
     near_rhs, near_q, shares = [], [], []
 
@@ -152,9 +144,10 @@
         column[...] = sq
         row[...] = jnp.transpose(jnp.broadcast_to(sq, (sq.shape[0], 128)))[0:1, :]
 
-    def tile(left, left_col, right_hl, right_lh, right_row):
+    def tile(left, left_col, right_hl, right_lh, right_row, factor=None):
         cross = dot(left, right_hl, LAST) + dot(left, right_lh, LAST)
-        return split(jnp.exp2((left_col + right_row) - (2.0 * SCALE) * cross))
+        t = jnp.exp2((left_col + right_row) - (2.0 * SCALE) * cross)
+        return split(t if factor is None else factor * t)
 
     def own_term(i, carry):
         rows = pl.ds(pl.multiple_of(i * BLOCK, BLOCK), BLOCK)
@@ -170,26 +163,19 @@
     for d in (2, 1, 3):
         other = lax.rem(chip + d, LEAVES // 2)
         piece.append(send(half.at[other, 1], pieces.at[chip], (2 * other + core, wide)))
-    own_rows = pl.ds(x * NZ, NZ)
-    arrived(skel_z)
-    skel_x = to_x_neighbours(skels.at[own_rows])
+    def set_of(d):
+        return skels.at[lax.rem(chip + d, LEAVES // 2), core]
+
+    arrived(skel_row)
+    skel_up = send(own_set, own_set, leaf_peer(2))
+    skel_down = send(own_set, own_set, leaf_peer(6))
+    skel_inside = [send(own_set, own_set, partner)]
     lax.fori_loop(0, STEPS, own_term, 0)
 
     arrived(piece)
-    coefs[wide] = jnp.sum(pieces[...], axis=0)
-    coef_z = along_z(coefs)
-    coef_x = {0: to_x_neighbours(coefs.at[wide])}
+    coefs[z] = jnp.sum(pieces[...], axis=0)
+    coef_row = {d: send(coefs.at[z], coefs.at[z], (leaf, z_index(d))) for d in FARTHEST_FIRST}
     send_rhs(2)
-    skel_x = passed_on(skel_x, skels.at[pl.ds(x_index(-way), NZ)])
-
-    def along_x(*offsets):
-        for d in offsets:
-            coef_z[d].wait_recv()
-            coef_x[d] = to_x_neighbours(coefs.at[z_index(-d)])
-
-    def onward(*offsets):
-        for d in offsets:
-            coef_x[d] = passed_on(coef_x[d], coefs.at[x_index(-way) + lax.rem(z - d + NZ, NZ)])
 
     arrived(near_q)
     high, low = split(q_in[...])
@@ -204,21 +190,61 @@
         shares.append(send(share_out.at[rows], share_in.at[rows], (leaf, behind)))
 
     share_term(0)
-    along_x(1, -1, 2, -2)
-    send_rhs(1)
+    skel_down.wait_recv()
+    skel_on = send(set_of(1), set_of(1), leaf_peer(6))
+    skel_inside.append(send(set_of(1), set_of(1), partner))
+    skel_up.wait_recv()
+    skel_inside.append(send(set_of(3), set_of(3), partner))
     share_term(1)
-    along_x(3, -3, 4)
-    send_rhs(2)
-    onward(0)
+    send_rhs(3)
     share_term(2)
-    onward(1, -1, 2, -2)
-
-    arrived(skel_x)
-    for j in range(FAR):
-        chosen[chip, core, j] = skels[far_ids[j, wide]]
-    picked = [send(chosen.at[chip, core], chosen.at[chip, core], leaf_peer(d)) for d in (2, 4, 6)]
     share_term(3)
-    onward(3, -3, 4)
+    skel_on.wait_recv()
+    skel_inside.append(send(set_of(2), set_of(2), partner))
+
+    arrived(skel_inside)
+    for i in range(NX):
+        points_of = skels[:, :, NZ + i].reshape(RANK, FEAT)
+        high, low = split(points_of)
+        rows = pl.ds(i * RANK, RANK)
+        far_hl[rows, 0:128], far_hl[rows, 128:256] = high, low
+        far_lh[rows, 0:128], far_lh[rows, 128:256] = low, high
+        far_points[rows, :] = points_of
+    norms(far_points, far_col, far_row)
+
+    def far_tile(i, carry):
+        sources = skels[:, :, i].reshape(RANK, FEAT)
+        source_sq = SCALE * jnp.sum(sources * sources, axis=1, keepdims=True)
+        lists = []
+        for k in range(NX):
+            hits = jnp.float32(0.0)
+            for j in range(FAR):
+                target = k * NZ + z
+                hit = (far_ids[j, target] == x * NZ + i) & (far_count[target] > j)
+                hits += jnp.where(hit, 1.0, 0.0).astype(F32)
+            lists.append(jnp.full((1, RANK), hits, F32))
+        tile_h[i], tile_l[i] = tile(
+            jnp.concatenate(split(sources), axis=1), source_sq, far_hl[...], far_lh[...], far_row[...],
+            jnp.concatenate(lists, axis=1))
+        return carry
+
+    lax.fori_loop(0, NZ, far_tile, 0)
+
+    def far_term(i):
+        high, low = split(coefs[i])
+        both = dot(jnp.concatenate([high, low], axis=0), tile_h[i])
+        return both[:PART] + (both[PART:] + dot(high, tile_l[i]))
+
+    total = far_term(z)
+    for d in FARTHEST_FIRST[::-1]:
+        coef_row[d].wait_recv()
+        total += far_term(lax.rem(z - d + NZ, NZ))
+    for i in range(NX):
+        parts_out[i] = total[:, i * RANK:(i + 1) * RANK]
+    parts = []
+    for d in (2, 1, 3):
+        parts.append(send(parts_out.at[lax.rem(x + d, NX)], parts_in.at[x], (leaf, x_index(d) + z)))
+    parts_in[x] = parts_out[x]
 
     first_id, second_id, used = near_ids[0, 0], near_ids[0, 1], near_count[0]
     number = leaf * WIDE + wide
@@ -237,32 +263,11 @@
         out[rows, :] += behind_used * dot3(t, (in_h[...], in_l[...]))
         return carry
 
-    lax.fori_loop(0, 2, near_term, 0)
-    arrived(picked)
-    picked = [send(chosen.at[:, core], chosen.at[:, core], (leaf - step, wide))]
-    lax.fori_loop(2, STEPS, near_term, 0)
-
-    arrived(picked + skel_leaf)
-    targets = skel_parent[...].reshape(RANK, FEAT)
-    target_high, target_low = split(targets)
-    target_hl = jnp.concatenate([target_high, target_low], axis=1)
-    target_lh = jnp.concatenate([target_low, target_high], axis=1)
-    target_sq = SCALE * jnp.sum(targets * targets, axis=1, keepdims=True)
-    target_row = jnp.transpose(jnp.broadcast_to(target_sq, (RANK, 128)))[0:1, :]
-    for j in range(FAR):
-        sources = chosen[:, :, j].reshape(RANK, FEAT)
-        source_sq = SCALE * jnp.sum(sources * sources, axis=1, keepdims=True)
-        tile_h[j], tile_l[j] = tile(
-            jnp.concatenate(split(sources), axis=1), source_sq, target_hl, target_lh, target_row)
-
-    for group in coef_x.values():
-        arrived(group)
-    total = jnp.zeros((PART, RANK), F32)
-    for j in range(FAR):
-        mask = jnp.where(far_count[wide] > j, 1.0, 0.0).astype(F32)
-        total += mask * dot3(split(coefs[far_ids[j, wide]]), (tile_h[j], tile_l[j]))
+    lax.fori_loop(0, STEPS, near_term, 0)
+
+    arrived(parts)
+    total = jnp.sum(parts_in[...], axis=0)
     field[chip, core] = total
-    partner = (leaf - step, wide)
     fields = [send(field.at[chip, core], field.at[chip, core], leaf_peer(d)) for d in (4, 2, 6)]
     inside = [send(field.at[chip, core], field.at[chip, core], partner)]
     arrived(shares)
@@ -299,10 +304,11 @@
             held(ROWS, COLS), wide_bf16, wide_bf16,
             held(ROWS, COLS), held(ROWS, COLS),
             held(LEAVES // 2, 2, PART, RANK), held(LEAVES // 2, 2, PART, RANK),
-            held(LEAVES // 2, PART, RANK), held(WIDE, PART, RANK),
-            held(LEAVES, PART, FEAT), held(WIDE, PART, FEAT),
-            held(LEAVES // 2, 2, FAR, PART, FEAT),
-            held(FAR, RANK, RANK, dtype=BF16), held(FAR, RANK, RANK, dtype=BF16),
+            held(LEAVES // 2, PART, RANK), held(NZ, PART, RANK),
+            held(LEAVES // 2, 2, NZ + NX, PART, FEAT),
+            held(NX * RANK, FEAT), wide_bf16, wide_bf16, held(ROWS, 1), held(1, ROWS),
+            held(NZ, RANK, NX * RANK, dtype=BF16), held(NZ, RANK, NX * RANK, dtype=BF16),
+            held(NX, PART, RANK), held(NX, PART, RANK),
             held(LEAVES // 2, 2, PART, RANK),
             pltpu.SemaphoreType.DMA((4,)),
             pltpu.SemaphoreType.DMA((COPIES,)),

time: 69.4 us -> 65.3 us (0.941)
  Pallas kernels: 65.9 us -> 61.8 us
    pallas_call x1, Pallas kernels: 65.9 us -> 61.8 us  [shards(): pl.pallas_call(kernel, out_shape=(jax.ShapeDtypeStruct((ROWS, COLS), F32)...]
where the time goes in v3:
time: 65.3 us; the launch traced here: 65.1 us
  Pallas kernels  61.8 us (95%)
  other arithmetic  2.65 us (4%)
  between operations  0.66 us (1%)
    pallas_call x1, Pallas kernels, shards(): pl.pallas_call(kernel, out_shape=(jax.ShapeDtypeStruct((ROWS, COLS), F32)...  61.8 us
    add x1, other arithmetic, shards(): return total + share  2.65 us

profile of v3, /device:TPU:1, one launch (start us, length us, event | category | flops | bytes accessed | tf_op | source)
XLA Modules:
  0.0 65.1 jit_solution(7528025829511037090)
XLA Ops:
  0.7 61.8 %shard_map.100 = (f32[1024,256]{1,0:T(8,128)}, f32[1024,256]{1,0:T(8,128)}) custom-call(s32[1,1024]{1,0:T(1,128)} %bitcast.2, s32[6,32]{1,0:T(8,128)} %bitcast.3, s32[32]{0:T(128)} %far_count.1, s32[1,2]{1,0:T(1,128)} %near_ids.1, s32[1]{0:T(128)S(6)} %copy.11.near_count, f32[1024,256]{1,0:T(8,128)} %rhs_hbm.1, f32[1024,128]{1,0:T(8,128)} %points_hbm.1, ...), custom_call_target="tpu_custom_call" | custom-call | tf_op jit(solution)/shard_map/pallas_call | solution.py:293
  62.4 2.6 %add.3 = f32[1024,256]{1,0:T(8,128)} add(f32[1024,256]{1,0:T(8,128)} %get-tuple-element.7, f32[1024,256]{1,0:T(8,128)} %get-tuple-element.8) | non-fusion elementwise | flops 262144 | bytes 3145728 | tf_op jit(solution)/shard_map/add | solution.py:320

commit v4 on v3

--- a/solution.py
+++ b/solution.py
@@ -37,12 +37,12 @@
 
 def kernel(
     order, far_ids, far_count, near_ids, near_count, rhs_hbm, points_hbm, basis_hbm, transfer_hbm, skeleton,
-    out, share,
+    out, share_in, field, transfer_out, basis_h, basis_l, used_out,
     rhs, points, basis, transfer,
     moved, q, own_hl, own_lh, own_col, own_row, q_in, in_hl, in_lh, in_col, in_row,
-    basis_h, basis_l, rhs_h, rhs_l, rhs_in, in_h, in_l, share_out, share_in,
+    rhs_h, rhs_l, rhs_in, in_h, in_l, share_out,
     lifted, half, pieces, coefs, skels, far_points, far_hl, far_lh, far_col, far_row, tile_h, tile_l,
-    parts_out, parts_in, field,
+    parts_out, parts_in,
     load_sems, send_sems, recv_sems,
 ):
     leaf, wide = lax.axis_index("leaf"), lax.axis_index("wide")
@@ -135,6 +135,7 @@
 
     leaf_coef = dot3((rhs_h[...], rhs_l[...]), (basis_h[...], basis_l[...]), FIRST)
     loads[3].wait()
+    transfer_out[...] = transfer[0]
     transfer_hl = split(transfer[0])
     lifted[...] = dot3(split(leaf_coef), transfer_hl).reshape(LEAVES // 2, 2, PART, RANK)
     halved = [send(lifted.at[:, 1 - core], half.at[:, 0], (leaf - step, wide))]
@@ -254,6 +255,7 @@
 
     behind_used, ahead_used = listed(number - step), listed(number + step)
 
+    used_out[...] = jnp.full(used_out.shape, ahead_used, F32)
     arrived(near_rhs)
     in_h[...], in_l[...] = split(rhs_in[...])
 
@@ -271,18 +273,29 @@
     fields = [send(field.at[chip, core], field.at[chip, core], leaf_peer(d)) for d in (4, 2, 6)]
     inside = [send(field.at[chip, core], field.at[chip, core], partner)]
     arrived(shares)
-    share[...] = ahead_used * share_in[...]
     for copy, d in ((fields[1], 2), (fields[2], 6), (fields[0], 4)):
         copy.wait_recv()
         block = field.at[lax.rem(chip + LEAVES // 2 - d // 2, LEAVES // 2), core]
         inside.append(send(block, block, partner))
     arrived(inside)
-    leaf_field = dot3(split(field[...].reshape(COLS, RANK)), transfer_hl, LAST)
-    out[...] += dot3((basis_h[...], basis_l[...]), split(leaf_field), LAST)
     for copy in copies:
         copy.wait_send()
 
 
+def finish(total, share, field, transfer, basis_h, basis_l, used, out, block, sems):
+    leaf_field = dot3(split(field[...].reshape(COLS, RANK)), split(transfer[...]), LAST)
+    leaf_field_hl = split(leaf_field)
+    copies = []
+    for i in range(STEPS):
+        rows = pl.ds(i * BLOCK, BLOCK)
+        far = dot3((basis_h[rows, :], basis_l[rows, :]), leaf_field_hl, LAST)
+        block[rows, :] = total[rows, :] + (far + used[0:1, 0:1] * share[rows, :])
+        copies.append(pltpu.make_async_copy(block.at[rows], out.at[rows], sems.at[i]))
+        copies[-1].start()
+    for copy in copies:
+        copy.wait()
+
+
 def shards(rhs, points, order, basis, transfer, skeleton, far_ids, far_count, near_ids, near_count):
     vmem, smem, anywhere = (pl.BlockSpec(memory_space=m) for m in (pltpu.VMEM, pltpu.SMEM, pl.ANY))
 
@@ -290,34 +303,43 @@
         return pltpu.VMEM(shape, dtype)
 
     wide_bf16 = held(ROWS, 256, dtype=BF16)
-    total, share = pl.pallas_call(
+    left = [
+        pltpu.VMEM((ROWS, COLS), F32), pltpu.VMEM((ROWS, COLS), F32), pltpu.VMEM((LEAVES // 2, 2, PART, RANK), F32),
+        pltpu.VMEM((RANK, RANK), F32), wide_bf16, wide_bf16, pltpu.VMEM((8, 128), F32)]
+    pieces = pl.pallas_call(
         kernel,
-        out_shape=(jax.ShapeDtypeStruct((ROWS, COLS), F32), jax.ShapeDtypeStruct((ROWS, COLS), F32)),
+        out_shape=left,
         in_specs=[vmem, smem, smem, smem, smem] + [anywhere] * 4 + [vmem],
-        out_specs=(vmem, vmem),
+        out_specs=[vmem] * len(left),
         scratch_shapes=[
             held(ROWS, COLS), held(ROWS, FEAT), held(ROWS, RANK), held(1, RANK, RANK),
             held(ROWS, 768, dtype=BF16),
             held(ROWS, FEAT), wide_bf16, wide_bf16, held(ROWS, 1), held(1, ROWS),
             held(ROWS, FEAT), wide_bf16, wide_bf16, held(ROWS, 1), held(1, ROWS),
-            wide_bf16, wide_bf16, wide_bf16, wide_bf16,
+            wide_bf16, wide_bf16,
             held(ROWS, COLS), wide_bf16, wide_bf16,
-            held(ROWS, COLS), held(ROWS, COLS),
+            held(ROWS, COLS),
             held(LEAVES // 2, 2, PART, RANK), held(LEAVES // 2, 2, PART, RANK),
             held(LEAVES // 2, PART, RANK), held(NZ, PART, RANK),
             held(LEAVES // 2, 2, NZ + NX, PART, FEAT),
             held(NX * RANK, FEAT), wide_bf16, wide_bf16, held(ROWS, 1), held(1, ROWS),
             held(NZ, RANK, NX * RANK, dtype=BF16), held(NZ, RANK, NX * RANK, dtype=BF16),
             held(NX, PART, RANK), held(NX, PART, RANK),
-            held(LEAVES // 2, 2, PART, RANK),
             pltpu.SemaphoreType.DMA((4,)),
             pltpu.SemaphoreType.DMA((COPIES,)),
             pltpu.SemaphoreType.DMA((COPIES,)),
         ],
         compiler_params=pltpu.CompilerParams(
-            collective_id=0, has_side_effects=True, vmem_limit_bytes=56 * 1024 * 1024),
+            collective_id=0, has_side_effects=True, vmem_limit_bytes=63000000),
     )(order.reshape(1, ROWS), far_ids.T, far_count, near_ids, near_count, rhs, points, basis, transfer, skeleton)
-    return total + share
+    return pl.pallas_call(
+        finish,
+        out_shape=jax.ShapeDtypeStruct((ROWS, COLS), F32),
+        in_specs=[vmem] * len(left),
+        out_specs=anywhere,
+        scratch_shapes=[held(ROWS, COLS), pltpu.SemaphoreType.DMA((STEPS,))],
+        compiler_params=pltpu.CompilerParams(vmem_limit_bytes=16 * 1024 * 1024),
+    )(*[pltpu.with_memory_space_constraint(piece, pltpu.VMEM) for piece in pieces])
 
 
 def solution(mesh):

time: 65.3 us -> 61.9 us (0.948)
  other arithmetic: 2.65 us -> 0 us
  Pallas kernels: 61.8 us -> 61.1 us
    add x1 -> x0, other arithmetic: 2.65 us -> none  [shards(): return total + share]
    pallas_call x1 -> x2, Pallas kernels: 61.8 us -> 61.1 us  [the longest x1 59.3 us: shards(): pl.pallas_call(kernel, out_shape=left, in_specs=[vmem, smem, smem, smem,...]
where the time goes in v4:
time: 61.9 us; the launch traced here: 61.7 us
  Pallas kernels  61.1 us (99%)
  between operations  0.66 us (1%)
    pallas_call x1, Pallas kernels, shards(): pl.pallas_call(kernel, out_shape=left, in_specs=[vmem, smem, smem, smem,...  59.3 us
    pallas_call x1, Pallas kernels, shards(): pl.pallas_call(finish, out_shape=jax.ShapeDtypeStruct((ROWS, COLS), F32),...  1.78 us

profile of v4, /device:TPU:1, one launch (start us, length us, event | category | flops | bytes accessed | tf_op | source)
XLA Modules:
  0.0 61.7 jit_solution(16698197180734158653)
XLA Ops:
  0.7 59.3 %shard_map.100 = (f32[1024,256]{1,0:T(8,128)S(1)}, f32[1024,256]{1,0:T(8,128)S(1)}, f32[4,2,32,256]{3,2,1,0:T(8,128)S(1)}, f32[256,256]{1,0:T(8,128)S(1)}, bf16[...) custom-call(s32[1,1024]{1,0:T(1,128)} %bitcast.2, s32[6,32]{1,0:T(8,128)} %bitcast.3, ...), custom_call_target="tpu_custom_call" | custom-call | tf_op jit(solution)/shard_map/pallas_call | solution.py:309
  59.9 1.8 %shard_map.101 = f32[1024,256]{1,0:T(8,128)} custom-call(f32[1024,256]{1,0:T(8,128)S(1)} %get-tuple-element.12.total, f32[1024,256]{1,0:T(8,128)S(1)} %get-tuple-element.13.share, f32[4,2,32,256]{3,2,1,0:T(8,128)S(1)} %get-tuple-element.14.field, f32[256,256]{1,0:T(8,128)S(1)} %get-tuple-element.15.transfer, ...), custom_call_target="tpu_custom_call" | custom-call | tf_op jit(solution)/shard_map/pallas_call | solution.py:335

commit v5 on v4

--- a/solution.py
+++ b/solution.py
@@ -19,7 +19,7 @@
 LAST = (((1,), (1,)), ((), ()))
 FIRST = (((0,), (0,)), ((), ()))
 PLAIN = (((1,), (0,)), ((), ()))
-FARTHEST_FIRST = (4, 3, -3, 2, -2, 1, -1)
+FARTHEST_FIRST = (-2, 3, -3, 2, 1, -1)
 
 
 def dot(a, b, dims=PLAIN):
@@ -88,11 +88,10 @@
         for copy in group:
             copy.wait_recv()
 
-    FARTHEST_FIRST = (4, 3, -3, 2, -2, 1, -1)
 
     own_set = skels.at[chip, core]
     partner = (leaf - step, wide)
-    skel_row = [send(skeleton.at[0], own_set.at[z], (leaf, z_index(d))) for d in FARTHEST_FIRST]
+    skel_row = [send(skeleton.at[0], own_set.at[z], (leaf, z_index(d))) for d in (4,) + FARTHEST_FIRST]
     skel_row += [send(skeleton.at[0], own_set.at[NZ + x], (leaf, x_index(d) + z)) for d in (2, 1, 3)]
     skels[chip, core, z] = skeleton[0]
     skels[chip, core, NZ + x] = skeleton[0]
@@ -191,6 +190,9 @@
         shares.append(send(share_out.at[rows], share_in.at[rows], (leaf, behind)))
 
     share_term(0)
+    coef_row[-2].wait_recv()
+    block = coefs.at[lax.rem(z + 2, NZ)]
+    coef_row[4] = send(block, block, (leaf, z_index(-2)))
     skel_down.wait_recv()
     skel_on = send(set_of(1), set_of(1), leaf_peer(6))
     skel_inside.append(send(set_of(1), set_of(1), partner))
@@ -237,8 +239,9 @@
         return both[:PART] + (both[PART:] + dot(high, tile_l[i]))
 
     total = far_term(z)
-    for d in FARTHEST_FIRST[::-1]:
-        coef_row[d].wait_recv()
+    for d in (-2, 1, -1, 2, 3, -3, 4):
+        if d != -2:
+            coef_row[d].wait_recv()
         total += far_term(lax.rem(z - d + NZ, NZ))
     for i in range(NX):
         parts_out[i] = total[:, i * RANK:(i + 1) * RANK]

time: 61.9 us -> 60.5 us (0.977)
  Pallas kernels: 61.1 us -> 59.7 us
    pallas_call x1, Pallas kernels: 59.3 us -> 57.9 us  [shards(): pl.pallas_call(kernel, out_shape=left, in_specs=[vmem, smem, smem, smem,...]
where the time goes in v5:
time: 60.5 us; the launch traced here: 60.3 us
  Pallas kernels  59.7 us (99%)
  between operations  0.66 us (1%)
    pallas_call x1, Pallas kernels, shards(): pl.pallas_call(kernel, out_shape=left, in_specs=[vmem, smem, smem, smem,...  57.9 us
    pallas_call x1, Pallas kernels, shards(): pl.pallas_call(finish, out_shape=jax.ShapeDtypeStruct((ROWS, COLS), F32),...  1.78 us

profile of v5, /device:TPU:1, one launch (start us, length us, event | category | flops | bytes accessed | tf_op | source)
XLA Modules:
  0.0 60.3 jit_solution(14624084846633183726)
XLA Ops:
  0.7 57.9 %shard_map.100 = (f32[1024,256]{1,0:T(8,128)S(1)}, f32[1024,256]{1,0:T(8,128)S(1)}, f32[4,2,32,256]{3,2,1,0:T(8,128)S(1)}, f32[256,256]{1,0:T(8,128)S(1)}, bf16[...) custom-call(s32[1,1024]{1,0:T(1,128)} %bitcast.2, s32[6,32]{1,0:T(8,128)} %bitcast.3, ...), custom_call_target="tpu_custom_call" | custom-call | tf_op jit(solution)/shard_map/pallas_call | solution.py:312
  58.5 1.8 %shard_map.101 = f32[1024,256]{1,0:T(8,128)} custom-call(f32[1024,256]{1,0:T(8,128)S(1)} %get-tuple-element.12.total, f32[1024,256]{1,0:T(8,128)S(1)} %get-tuple-element.13.share, f32[4,2,32,256]{3,2,1,0:T(8,128)S(1)} %get-tuple-element.14.field, f32[256,256]{1,0:T(8,128)S(1)} %get-tuple-element.15.transfer, ...), custom_call_target="tpu_custom_call" | custom-call | tf_op jit(solution)/shard_map/pallas_call | solution.py:338
